TPU v7x, 32 devices: a whole 2x2x4 slice. The times are simulated.
32 devices in a mesh: dp: 16 (over z, x, core), rows: 2 (over y).
Axes of the slice: x: 2, y: 2, z: 4, core: 2. Of those that a mesh axis runs over, the one named last changes fastest.
Arguments:
- fine_level: bfloat16 [16, 32, 64, 256], P('dp', 'rows'), may hold values from -6 to 6
- out_grad: bfloat16 [16, 32, 64, 256], P('dp', 'rows'), may hold values from -6 to 6
- fine_input: bfloat16 [16, 32, 64, 256], P('dp', 'rows'), may hold values from -6 to 6
- mid_input: bfloat16 [16, 16, 32, 512], P('dp', None, None, 'rows'), may hold values from -6 to 6
- top_input: bfloat16 [16, 8, 16, 1024], P('dp', None, None, 'rows'), may hold values from -6 to 6
- smooth_weight: bfloat16 [3, 3, 256, 256], replicated, may hold values from -0.125 to 0.125
- fine_lateral: bfloat16 [256, 256], replicated, may hold values from -0.375 to 0.375
- mid_lateral: bfloat16 [512, 256], P('rows'), may hold values from -0.375 to 0.375
- top_lateral: bfloat16 [1024, 256], P('rows'), may hold values from -0.375 to 0.375
Outputs:
- grad_fine: bfloat16 [16, 32, 64, 256], P('dp', 'rows')
- grad_mid: bfloat16 [16, 16, 32, 512], P('dp', None, None, 'rows')
- grad_top: bfloat16 [16, 8, 16, 1024], P('dp', None, None, 'rows')
- kernel_grads: float32 [2560, 256], P('dp')
- midlat_grad: float32 [512, 256], P('rows')
- toplat_grad: float32 [1024, 256], P('rows')
All inputs are finite; a program needn't handle non-finite values.
Results may differ from a plain program's by a relative error of at most 0.0062.
Values may be sent and summed in bfloat16 or wider, within the bound.
A program may use at most 64 MiB of HBM per device.

v0:
```python
import functools

import jax
import jax.numpy as jnp
from jax import lax
from jax.experimental import pallas as pl
from jax.experimental.pallas import tpu as pltpu
from jax.sharding import PartitionSpec as P

BF = jnp.bfloat16
F32 = jnp.float32
MESH = pl.DeviceIdType.MESH


def with_halo(value, sides, width):
    for axis, dim in sides:
        count, length = (lax.axis_size(axis), value.shape[dim])
        up = [(i, (i + 1) % count) for i in range(count - 1)]
        down = [(j, i) for i, j in up]
        last = lax.slice_in_dim(value, length - width, length, axis=dim)
        leading = lax.slice_in_dim(value, 0, width, axis=dim)
        before = lax.ppermute(last, axis, up)
        after = lax.ppermute(leading, axis, down)
        value = jnp.concatenate([before, value, after], axis=dim)
    return value


def pool_two(field):
    images, rows_n, cols_n, chans = field.shape
    return field.reshape(images, rows_n // 2, 2, cols_n // 2, 2, chans).sum(axis=(2, 4))


def contract_last(left, right):
    return lax.dot_general(
        left, right, (((1,), (1,)), ((), ())), preferred_element_type=jnp.float32
    )


def contract_first(left, right):
    return lax.dot_general(
        left, right, (((0,), (0,)), ((), ())), preferred_element_type=jnp.float32
    )


def plain_body(
    fine_level,
    out_grad,
    fine_input,
    mid_input,
    top_input,
    smooth_weight,
    fine_lateral,
    mid_lateral,
    top_lateral,
):
    images, strip, width, chans = out_grad.shape
    cells = images * strip * width
    rimmed = with_halo(out_grad, (("rows", 1),), 1)
    rimmed = jnp.pad(rimmed, ((0, 0), (0, 0), (1, 1), (0, 0)))
    fine_flat = fine_level.reshape(cells, chans)
    level_grad = jnp.zeros((cells, chans), jnp.float32)
    pieces = []
    for tap_a in range(3):
        for tap_b in range(3):
            shifted = rimmed[
                :, 2 - tap_a : 2 - tap_a + strip, 2 - tap_b : 2 - tap_b + width, :
            ].reshape(cells, chans)
            level_grad = level_grad + contract_last(shifted, smooth_weight[tap_a, tap_b])
            pieces.append(contract_first(fine_flat, shifted))
    fine_grad = level_grad.astype(jnp.bfloat16)
    grad_fine = (
        contract_last(fine_grad, fine_lateral)
        .astype(jnp.bfloat16)
        .reshape(images, strip, width, -1)
    )
    pieces.append(contract_first(fine_input.reshape(cells, -1), fine_grad))
    kernel_term = jnp.concatenate(pieces, axis=0)
    share = lax.psum_scatter(kernel_term, "dp", scatter_dimension=0, tiled=True)
    kernel_grads = lax.psum(share, "rows")
    pooled = pool_two(level_grad.reshape(images, strip, width, chans)).astype(jnp.bfloat16)
    mid_grad = lax.all_gather(pooled, "rows", axis=1, tiled=True)
    top_grad = pool_two(mid_grad.astype(jnp.float32)).astype(jnp.bfloat16)
    mid_flat = mid_grad.reshape(-1, chans)
    top_flat = top_grad.reshape(-1, chans)
    grad_mid = contract_last(mid_flat, mid_lateral).astype(jnp.bfloat16).reshape(mid_input.shape)
    grad_top = contract_last(top_flat, top_lateral).astype(jnp.bfloat16).reshape(top_input.shape)
    mid_term = contract_first(mid_input.reshape(mid_flat.shape[0], -1), mid_flat)
    top_term = contract_first(top_input.reshape(top_flat.shape[0], -1), top_flat)
    midlat_grad, toplat_grad = lax.psum((mid_term, top_term), "dp")
    return (grad_fine, grad_mid, grad_top, kernel_grads, midlat_grad, toplat_grad)


def rows_of(start, size, step):
    return pl.ds(pl.multiple_of(start, step), size)


def fused(
    nz, nx, nr, strip, width,
    fl_h, og_h, fi_h, mi_h, ti_h, w_h, lf_h, lm_h, lt_h,
    gf_h, gm_h, gt_h, kf_h, ga_h,
    og, fine, fin, mid_in, top_in, wcat, lat_f, lat_m, lat_t,
    halo, taps, acc, fg, pool_f, midg, topf, topg,
    kgb, ra, sb, rb, tb, rc, kf,
    ct, rca, sc, rcs, gath,
    gf, gm, gt,
    in_sem, w_sem, out_sem, halo_s, halo_r, mid_s, mid_r,
    a_s, a_r, b_s, b_r, c_s, c_r, d_s, d_r,
    ca_s, ca_r, cs_s, cs_r, cg_s, cg_r, cc_s, cc_r,
):
    chips = nz * nx
    d = lax.axis_index("dp")
    r = lax.axis_index("rows")
    core = lax.rem(d, 2)
    q = d // 2
    x = lax.rem(q, nx)
    z = q // nx
    other = 1 - core
    sibling = (q * 2 + other, r)
    cells, chans = og.shape
    share = kf.shape[0]
    part = share // nr

    def dev(z1, x1, r1):
        return ((z1 * nx + x1) * 2 + core, r1)

    def remote(src, dst, ss, rs, to):
        return pltpu.make_async_remote_copy(
            src_ref=src, dst_ref=dst, send_sem=ss, recv_sem=rs,
            device_id=to, device_id_type=MESH,
        )

    loads = []
    for n, (src, dst) in enumerate(
        ((og_h, og), (fl_h, fine), (fi_h, fin), (lf_h, lat_f), (mi_h, mid_in),
         (ti_h, top_in), (lm_h, lat_m), (lt_h, lat_t))
    ):
        loads.append(pltpu.make_async_copy(src, dst, in_sem.at[n]))
    wloads = []
    for a in range(3):
        for b in range(3):
            wloads.append(pltpu.make_async_copy(
                w_h.at[a, b], wcat.at[a, :, b * chans:(b + 1) * chans], w_sem.at[3 * a + b]
            ))
    loads[0].start()
    for cp in wloads:
        cp.start()
    for cp in loads[1:]:
        cp.start()

    barrier = pltpu.get_barrier_semaphore()
    plane = [(i, j) for i in range(nx) for j in range(nr) if (i, j) != (0, 0)]
    greet = [sibling]
    for k in range(1, chips):
        greet.append((lax.rem(q + k, chips) * 2 + core, r))
    for i, j in plane:
        if j:
            greet.append(dev(z, lax.rem(x + i, nx), lax.rem(r + j, nr)))
    for to in greet:
        pl.semaphore_signal(barrier, inc=1, device_id=to, device_id_type=MESH)

    loads[0].wait()
    pl.semaphore_wait(barrier, len(greet))
    down = remote(og.at[pl.ds(cells - width, width)], halo.at[0], halo_s.at[0], halo_r.at[0],
                  (d, lax.rem(r + 1, nr)))
    up = remote(og.at[pl.ds(0, width)], halo.at[1], halo_s.at[1], halo_r.at[1],
                (d, lax.rem(r + nr - 1, nr)))

    @pl.when(r < nr - 1)
    def _():
        down.start()

    @pl.when(r > 0)
    def _():
        up.start()

    col = lax.broadcasted_iota(jnp.int32, (width, chans), 0)

    def spread(value, at):
        wide = value.astype(F32)
        after = jnp.where(col == width - 1, 0.0, pltpu.roll(wide, width - 1, 0))
        before = jnp.where(col == 0, 0.0, pltpu.roll(wide, 1, 0))
        here = pl.ds(at * width, width)
        taps[here, 0:chans] = after.astype(BF)
        taps[here, chans:2 * chans] = value
        taps[here, 2 * chans:3 * chans] = before.astype(BF)

    for y in range(strip):
        spread(og[pl.ds(y * width, width), :], y + 1)
    for cp in wloads:
        cp.wait()

    def shifted(a):
        return taps[pl.ds((2 - a) * width, cells), :]

    acc[...] = contract_last(shifted(1), wcat[1])

    @pl.when(r > 0)
    def _():
        down.wait_recv()

    @pl.when(r == 0)
    def _():
        halo[0] = jnp.zeros_like(halo[0])

    @pl.when(r < nr - 1)
    def _():
        up.wait_recv()

    @pl.when(r == nr - 1)
    def _():
        halo[1] = jnp.zeros_like(halo[1])

    spread(halo[0], 0)
    spread(halo[1], strip + 1)
    acc[...] += contract_last(shifted(0), wcat[0])
    acc[...] += contract_last(shifted(2), wcat[2])

    half = width // 2
    lanes = [pl.ds(v * 128, 128) for v in range(chans // 128)]
    for y in range(strip // 2):
        pair = acc[pl.ds(2 * y * width, width), :] + acc[pl.ds((2 * y + 1) * width, width), :]
        for v in range(chans // 128):
            pool_f[v, pl.ds(y * width, width), :] = pair[:, v * 128:(v + 1) * 128]
    mine = cells // 4
    for v, lane in enumerate(lanes):
        midg[r, :, lane] = (
            pool_f[v, pl.ds(0, mine, stride=2), :] + pool_f[v, pl.ds(1, mine, stride=2), :]
        ).astype(BF)
    mids = []
    for j in range(1, nr):
        cp = remote(midg.at[r], midg.at[r], mid_s.at[j - 1], mid_r.at[j - 1],
                    (d, lax.rem(r + j, nr)))
        cp.start()
        mids.append(cp)
    fg[...] = acc[...].astype(BF)

    loads[1].wait()
    fine_t = fine[...].T
    for a in range(3):
        got = jnp.dot(fine_t, shifted(a), preferred_element_type=F32).astype(BF)
        for b in range(3):
            kgb[pl.ds((3 * a + b) * chans, chans), :] = got[:, b * chans:(b + 1) * chans]
    loads[2].wait()
    kgb[pl.ds(9 * chans, fin.shape[1]), :] = jnp.dot(
        fin[...].T, fg[...], preferred_element_type=F32
    ).astype(BF)
    firsts = []
    for n in range(chips):
        cp = remote(kgb.at[rows_of((2 * n + other) * share, share, 16)], ra.at[n],
                    a_s.at[n], a_r.at[n], sibling)
        cp.start()
        firsts.append(cp)

    for cp in mids:
        cp.wait_recv()
    loads[4].wait()
    loads[5].wait()
    hw = half
    for t in range(nr):
        for y in range(strip // 4):
            pair = (
                midg[t, pl.ds(2 * y * hw, hw), :].astype(F32)
                + midg[t, pl.ds((2 * y + 1) * hw, hw), :].astype(F32)
            )
            for v in range(chans // 128):
                topf[v, pl.ds((t * (strip // 4) + y) * hw, hw), :] = pair[:, v * 128:(v + 1) * 128]
    tops = topg.shape[0]
    for v, lane in enumerate(lanes):
        topg[:, lane] = (
            topf[v, pl.ds(0, tops, stride=2), :] + topf[v, pl.ds(1, tops, stride=2), :]
        ).astype(BF)
    mflat = midg[...].reshape(nr * mine, chans)
    mc, tc = mid_in.shape[1], top_in.shape[1]
    ct[pl.ds(0, mc), :] = jnp.dot(
        mid_in[...].T, mflat, preferred_element_type=F32).astype(BF)
    ct[pl.ds(mc, tc), :] = jnp.dot(
        top_in[...].T, topg[...], preferred_element_type=F32).astype(BF)
    per = sc.shape[0]
    chunk = per // chips
    cfirst = remote(ct.at[rows_of(other * per, per, 16)], rca, ca_s, ca_r, sibling)
    cfirst.start()

    for n in range(chips):
        firsts[n].wait_recv()
        sb[n] = (
            kgb[rows_of((2 * n + core) * share, share, 16), :].astype(F32) + ra[n].astype(F32)
        ).astype(BF)

    cfirst.wait_recv()
    sc[...] = (
        ct[rows_of(core * per, per, 16), :].astype(F32) + rca[...].astype(F32)
    ).astype(BF)
    cscat = []
    for k in range(1, chips):
        to = lax.rem(q + k, chips)
        cp = remote(sc.at[rows_of(to * chunk, chunk, 16)], rcs.at[k - 1],
                    cs_s.at[k - 1], cs_r.at[k - 1], (to * 2 + core, r))
        cp.start()
        cscat.append(cp)

    order = list(range(1, nz)) + [0]
    seconds = []
    for t in order:
        zt = lax.rem(z + t, nz)
        row = []
        for n, (i, j) in enumerate(plane):
            xt, rt = lax.rem(x + i, nx), lax.rem(r + j, nr)
            cp = remote(sb.at[zt * nx + xt, rows_of(rt * part, part, 16)], rb.at[n, t],
                        b_s.at[n, t], b_r.at[n, t], dev(z, xt, rt))
            cp.start()
            row.append(cp)
        seconds.append((t, zt, row))

    loads[3].wait()
    gf[...] = contract_last(fg[...], lat_f[...]).astype(BF)
    outs = [pltpu.make_async_copy(gf, gf_h, out_sem.at[0])]
    outs[0].start()
    loads[6].wait()
    gm[...] = contract_last(mflat, lat_m[...]).astype(BF)
    outs.append(pltpu.make_async_copy(gm, gm_h, out_sem.at[1]))
    outs[1].start()
    loads[7].wait()
    gt[...] = contract_last(topg[...], lat_t[...]).astype(BF)
    outs.append(pltpu.make_async_copy(gt, gt_h, out_sem.at[2]))
    outs[2].start()

    total = sc[rows_of(q * chunk, chunk, 16), :].astype(F32)
    for k in range(1, chips):
        cscat[k - 1].wait_recv()
        total += rcs[k - 1].astype(F32)
    place = core * per + q * chunk
    gath[rows_of(place, chunk, 16), :] = total.astype(BF)
    cgath = []
    for k in range(1, chips):
        here = rows_of(place, chunk, 16)
        cp = remote(gath.at[here], gath.at[here], cg_s.at[k - 1], cg_r.at[k - 1],
                    (lax.rem(q + k, chips) * 2 + core, r))
        cp.start()
        cgath.append(cp)

    thirds = []
    for t, zt, row in seconds:
        total = sb[zt * nx + x, rows_of(r * part, part, 16), :].astype(F32)
        for n, cp in enumerate(row):
            cp.wait_recv()
            total += rb[n, t].astype(F32)
        if t:
            tb[t - 1] = total.astype(BF)
            cp = remote(tb.at[t - 1], rc.at[t - 1], c_s.at[t - 1], c_r.at[t - 1],
                        dev(zt, x, r))
            cp.start()
            thirds.append(cp)
    for n, cp in enumerate(thirds):
        cp.wait_recv()
        total += rc[n].astype(F32)
    spot = rows_of(r * part, part, 16)
    kf[spot, :] = total.astype(BF)
    lasts = []
    for j in range(1, nr):
        cp = remote(kf.at[spot], kf.at[spot], d_s.at[j - 1], d_r.at[j - 1],
                    (d, lax.rem(r + j, nr)))
        cp.start()
        lasts.append(cp)

    for cp in cgath:
        cp.wait_recv()
    block = rows_of(core * per, per, 16)
    ccore = remote(gath.at[block], gath.at[block], cc_s, cc_r, sibling)
    ccore.start()
    for cp in lasts:
        cp.wait_recv()
    outs.append(pltpu.make_async_copy(kf, kf_h, out_sem.at[3]))
    outs[3].start()
    ccore.wait_recv()
    outs.append(pltpu.make_async_copy(gath, ga_h, out_sem.at[4]))
    outs[4].start()

    @pl.when(r < nr - 1)
    def _():
        down.wait_send()

    @pl.when(r > 0)
    def _():
        up.wait_send()

    sent = mids + firsts + [cfirst] + cscat + cgath + thirds + lasts + [ccore]
    for _, _, row in seconds:
        sent += row
    for cp in sent:
        cp.wait_send()
    for cp in outs:
        cp.wait()


def put_out(gf_i, gm_i, gt_i, kf_i, ga_i, gf_o, gm_o, gt_o, kg_o, ml_o, tl_o,
            kf, ga, kg, ml, tl, in_sem, out_sem):
    loads = [
        pltpu.make_async_copy(src, dst, in_sem.at[n])
        for n, (src, dst) in enumerate(
            ((ga_i, ga), (kf_i, kf)))
    ]
    for cp in loads:
        cp.start()
    stores = [
        pltpu.make_async_copy(src, dst, out_sem.at[n])
        for n, (src, dst) in enumerate(
            ((gf_i, gf_o), (gm_i, gm_o), (gt_i, gt_o), (kg, kg_o), (ml, ml_o), (tl, tl_o)))
    ]
    for n in range(3):
        stores[n].start()
    loads[1].wait()
    kg[...] = kf[...].astype(F32)
    stores[3].start()
    loads[0].wait()
    mc = ml.shape[0]
    ml[...] = ga[pl.ds(0, mc), :].astype(F32)
    stores[4].start()
    tl[...] = ga[pl.ds(mc, tl.shape[0]), :].astype(F32)
    stores[5].start()
    for cp in stores:
        cp.wait()


def kernel_body(nz, nx, nr, fine_level, out_grad, fine_input, mid_input, top_input,
                smooth_weight, fine_lateral, mid_lateral, top_lateral):
    _, strip, width, chans = out_grad.shape
    cells = strip * width
    cin = fine_input.shape[-1]
    mc, tc = mid_input.shape[-1], top_input.shape[-1]
    mcells = mid_input.shape[1] * mid_input.shape[2]
    tcells = top_input.shape[1] * top_input.shape[2]
    chips = nz * nx
    rows = 9 * chans + cin
    share = rows // (2 * chips)
    part = share // nr
    per = (mc + tc) // 2
    chunk = per // chips
    npl = nx * nr - 1
    dma = pltpu.SemaphoreType.DMA
    vm = pltpu.VMEM
    scratch = [
        vm((cells, chans), BF), vm((cells, chans), BF), vm((cells, cin), BF),
        vm((mcells, mc), BF), vm((tcells, tc), BF), vm((3, chans, 3 * chans), BF),
        vm((cin, chans), BF), vm((mc, chans), BF), vm((tc, chans), BF),
        vm((2, width, chans), BF), vm(((strip + 2) * width, 3 * chans), BF),
        vm((cells, chans), F32), vm((cells, chans), BF), vm((chans // 128, cells // 2, 128), F32),
        vm((nr, cells // 4, chans), BF), vm((chans // 128, mcells // 2, 128), F32), vm((tcells, chans), BF),
        vm((rows, chans), BF), vm((chips, share, chans), BF), vm((chips, share, chans), BF),
        vm((npl, nz, part, chans), BF), vm((nz - 1, part, chans), BF),
        vm((nz - 1, part, chans), BF), vm((share, chans), BF),
        vm((2 * per, chans), BF), vm((per, chans), BF), vm((per, chans), BF),
        vm((chips - 1, chunk, chans), BF), vm((2 * per, chans), BF),
        vm((cells, cin), BF), vm((mcells, mc), BF), vm((tcells, tc), BF),
        dma((8,)), dma((9,)), dma((5,)), dma((2,)), dma((2,)), dma((nr - 1,)), dma((nr - 1,)),
        dma((chips,)), dma((chips,)), dma((npl, nz)), dma((npl, nz)),
        dma((nz - 1,)), dma((nz - 1,)), dma((nr - 1,)), dma((nr - 1,)),
        dma(()), dma(()), dma((chips - 1,)), dma((chips - 1,)),
        dma((chips - 1,)), dma((chips - 1,)), dma(()), dma(()),
    ]
    hbm = pl.BlockSpec(memory_space=pltpu.HBM)
    anyspec = pl.BlockSpec(memory_space=pl.ANY)
    wide = [
        jax.ShapeDtypeStruct((cells, cin), BF), jax.ShapeDtypeStruct((mcells, mc), BF),
        jax.ShapeDtypeStruct((tcells, tc), BF),
    ]
    held = [jax.ShapeDtypeStruct((share, chans), BF), jax.ShapeDtypeStruct((2 * per, chans), BF)]
    final = [
        jax.ShapeDtypeStruct((share, chans), F32), jax.ShapeDtypeStruct((mc, chans), F32),
        jax.ShapeDtypeStruct((tc, chans), F32),
    ]
    whole = 67043328
    between = pl.pallas_call(
        functools.partial(fused, nz, nx, nr, strip, width),
        out_shape=[pltpu.VMEM(o.shape, o.dtype) for o in wide + held],
        in_specs=[hbm] * 9,
        out_specs=[anyspec] * 5,
        scratch_shapes=scratch,
        compiler_params=pltpu.CompilerParams(
            collective_id=0, has_side_effects=True, vmem_limit_bytes=48 * 1024 * 1024
        ),
    )(*(pltpu.with_memory_space_constraint(value, pltpu.HBM) for value in (
        fine_level.reshape(cells, chans), out_grad.reshape(cells, chans),
        fine_input.reshape(cells, cin), mid_input.reshape(mcells, mc),
        top_input.reshape(tcells, tc), smooth_weight, fine_lateral, mid_lateral, top_lateral,
    )))
    gf, gm, gt, kg, ml, tl = pl.pallas_call(
        put_out,
        out_shape=wide + final,
        in_specs=[anyspec] * 5,
        out_specs=[hbm] * 6,
        scratch_shapes=[vm(o.shape, o.dtype) for o in held + final]
        + [dma((2,)), dma((6,))],
        compiler_params=pltpu.CompilerParams(vmem_limit_bytes=8 * 1024 * 1024),
    )(*between)
    return (
        gf.reshape(fine_input.shape), gm.reshape(mid_input.shape),
        gt.reshape(top_input.shape), kg, ml, tl,
    )


def body(nr, *args):
    fine_level, out_grad, fine_input, mid_input, top_input = args[:5]
    dp = lax.axis_size("dp")
    chips = dp // 2
    nx = max((n for n in range(1, chips + 1) if chips % n == 0 and n * n <= chips), default=1)
    images, strip, width, chans = out_grad.shape
    rows = 9 * chans + fine_input.shape[-1]
    coarse = mid_input.shape[-1] + top_input.shape[-1]
    fits = (
        dp % 2 == 0 and images == 1 and nr > 1 and chips > nx
        and rows % (dp * nr * 16) == 0 and coarse % (dp * 16) == 0
        and strip % 4 == 0 and width % 64 == 0 and chans % 128 == 0
    )
    if not fits:
        return plain_body(*args)
    return kernel_body(chips // nx, nx, nr, *args)


def solution(mesh):
    placed = (
        P("dp", "rows", None, None),
        P("dp", "rows", None, None),
        P("dp", "rows", None, None),
        P("dp", None, None, "rows"),
        P("dp", None, None, "rows"),
        P(),
        P(),
        P("rows", None),
        P("rows", None),
    )
    return jax.shard_map(
        functools.partial(body, mesh.shape["rows"]),
        mesh=mesh,
        in_specs=placed,
        out_specs=(
            P("dp", "rows", None, None),
            P("dp", None, None, "rows"),
            P("dp", None, None, "rows"),
            P("dp", None),
            P("rows", None),
            P("rows", None),
        ),
        check_vma=False,
    )
```

profile of v0, /device:TPU:0, one launch (start us, length us, event | category | flops | bytes accessed | tf_op | source)
XLA Modules:
  0.0 36.4 jit_solution(174706070682811083)
XLA Ops:
  0.6 34.1 %shard_map.136 = (bf16[1024,256]{1,0:T(8,128)(2,1)S(1)}, bf16[512,256]{1,0:T(8,128)(2,1)S(1)}, bf16[128,512]{1,0:T(8,128)(2,1)S(1)}, bf16[160,256]{1,0:T(8,128)(2,1)S(1)}, bf16[768,256]{1,0:T(8,128)(2,1)S(1)}) custom-call(bf16[1024,256]{1,0:T(8,128)(2,1)} %bitcast.8, bf16[1024,256]{1,0:T(8,128)(2,1)} %bitcast.9, bf16[1024,256]{1,0:T(8,128)(2,1)} %bitcast.10, ...), custom_call_target="tpu_custom_call" | custom-call | tf_op jit(solution)/shard_map/pallas_call | solution.py:472
  34.8 1.6 %shard_map.137 = (bf16[1024,256]{1,0:T(8,128)(2,1)}, bf16[512,256]{1,0:T(8,128)(2,1)}, bf16[128,512]{1,0:T(8,128)(2,1)}, f32[160,256]{1,0:T(8,128)}, f32[256,256]{1,0:T(8,128)}, /*index=5*/f32[512,256]{1,0:T(8,128)}) custom-call(bf16[1024,256]{1,0:T(8,128)(2,1)S(1)} %get-tuple-element.17.gf_i, bf16[512,256]{1,0:T(8,128)(2,1)S(1)} %get-tuple-element.18.gm_i, ...), custom_call_target="tpu_custom_call" | custom-call | tf_op jit(solution)/shard_map/pallas_call | solution.py:486
where the time goes:
time: 36.5 us; the launch traced here: 36.4 us
  Pallas kernels  35.7 us (98%)
  between operations  0.64 us (2%)
    pallas_call x1, Pallas kernels, kernel_body(): pl.pallas_call(functools.partial(fused, nz, nx, nr, strip, width), out_sh...  34.1 us
    pallas_call x1, Pallas kernels, kernel_body(): pl.pallas_call(put_out, out_shape=wide + final, in_specs=[anyspec] * 5, o...  1.6 us

commit v1 on v0

--- a/solution.py
+++ b/solution.py
@@ -99,7 +99,7 @@
     fl_h, og_h, fi_h, mi_h, ti_h, w_h, lf_h, lm_h, lt_h,
     gf_h, gm_h, gt_h, kf_h, ga_h,
     og, fine, fin, mid_in, top_in, wcat, lat_f, lat_m, lat_t,
-    halo, taps, acc, fg, pool_f, midg, topf, topg,
+    halo, taps, ftr, acc, kacc, fg, pool_f, midg, topf, topg,
     kgb, ra, sb, rb, tb, rc, kf,
     ct, rca, sc, rcs, gath,
     gf, gm, gt,
@@ -131,8 +131,8 @@
 
     loads = []
     for n, (src, dst) in enumerate(
-        ((og_h, og), (fl_h, fine), (fi_h, fin), (lf_h, lat_f), (mi_h, mid_in),
-         (ti_h, top_in), (lm_h, lat_m), (lt_h, lat_t))
+        ((og_h, og), (fl_h, fine.at[pl.ds(width, cells)]), (fi_h, fin), (lf_h, lat_f),
+         (mi_h, mid_in), (ti_h, top_in), (lm_h, lat_m), (lt_h, lat_t))
     ):
         loads.append(pltpu.make_async_copy(src, dst, in_sem.at[n]))
     wloads = []
@@ -158,6 +158,22 @@
     for to in greet:
         pl.semaphore_signal(barrier, inc=1, device_id=to, device_id_type=MESH)
 
+    top_rim, low_rim = pl.ds(0, width), pl.ds((strip + 1) * width, width)
+    taps[top_rim, :] = jnp.zeros((width, 3 * chans), BF)
+    taps[low_rim, :] = jnp.zeros((width, 3 * chans), BF)
+    fine[top_rim, :] = jnp.zeros((width, chans), BF)
+    fine[low_rim, :] = jnp.zeros((width, chans), BF)
+
+    col = lax.broadcasted_iota(jnp.int32, (width, chans), 0)
+
+    def spread(value, here):
+        wide = value.astype(F32)
+        after = jnp.where(col == width - 1, 0.0, pltpu.roll(wide, width - 1, 0))
+        before = jnp.where(col == 0, 0.0, pltpu.roll(wide, 1, 0))
+        taps[here, 0:chans] = after.astype(BF)
+        taps[here, chans:2 * chans] = value
+        taps[here, 2 * chans:3 * chans] = before.astype(BF)
+
     loads[0].wait()
     pl.semaphore_wait(barrier, len(greet))
     down = remote(og.at[pl.ds(cells - width, width)], halo.at[0], halo_s.at[0], halo_r.at[0],
@@ -173,26 +189,71 @@
     def _():
         up.start()
 
-    col = lax.broadcasted_iota(jnp.int32, (width, chans), 0)
-
-    def spread(value, at):
-        wide = value.astype(F32)
-        after = jnp.where(col == width - 1, 0.0, pltpu.roll(wide, width - 1, 0))
-        before = jnp.where(col == 0, 0.0, pltpu.roll(wide, 1, 0))
-        here = pl.ds(at * width, width)
-        taps[here, 0:chans] = after.astype(BF)
-        taps[here, chans:2 * chans] = value
-        taps[here, 2 * chans:3 * chans] = before.astype(BF)
-
-    for y in range(strip):
-        spread(og[pl.ds(y * width, width), :], y + 1)
+    def spread_row(y, carry):
+        spread(og[rows_of(y * width, width, width), :], rows_of((y + 1) * width, width, width))
+        return carry
+
+    lax.fori_loop(0, strip, spread_row, 0)
     for cp in wloads:
         cp.wait()
 
-    def shifted(a):
-        return taps[pl.ds((2 - a) * width, cells), :]
-
-    acc[...] = contract_last(shifted(1), wcat[1])
+    level = contract_last(taps[pl.ds(2 * width, cells), :], wcat[0])
+    level += contract_last(taps[pl.ds(width, cells), :], wcat[1])
+    level += contract_last(taps[pl.ds(0, cells), :], wcat[2])
+    acc[...] = level
+
+    half = width // 2
+    mine = cells // 4
+    lanes = [pl.ds(v * 128, 128) for v in range(chans // 128)]
+
+    def pool(y0, count):
+        for y in range(y0, y0 + count):
+            pair = acc[pl.ds(2 * y * width, width), :] + acc[pl.ds((2 * y + 1) * width, width), :]
+            for v in range(chans // 128):
+                pool_f[v, pl.ds(y * width, width), :] = pair[:, v * 128:(v + 1) * 128]
+        for v, lane in enumerate(lanes):
+            midg[r, pl.ds(y0 * half, count * half), lane] = (
+                pool_f[v, pl.ds(y0 * width, count * half, stride=2), :]
+                + pool_f[v, pl.ds(y0 * width + 1, count * half, stride=2), :]
+            ).astype(BF)
+
+    mrows = strip // 2
+    pool(1, mrows - 2)
+    mids = []
+
+    def send_mid(e, y0, count):
+        here = midg.at[r, pl.ds(y0 * half, count * half)]
+        for j in range(1, nr):
+            cp = remote(here, here, mid_s.at[j - 1, e], mid_r.at[j - 1, e],
+                        (d, lax.rem(r + j, nr)))
+            cp.start()
+            mids.append(cp)
+
+    send_mid(0, 1, mrows - 2)
+
+    inner = pl.ds(width, cells - 2 * width)
+    fg[inner, :] = acc[inner, :].astype(BF)
+
+    loads[1].wait()
+    wide_t = fine[...].T
+    ftr[pl.ds(0, chans), :] = wide_t[:, 0:cells]
+    ftr[pl.ds(chans, chans), :] = fine[pl.ds(width, cells), :].T
+    ftr[pl.ds(2 * chans, chans), :] = wide_t[:, 2 * width:2 * width + cells]
+
+    def ktap(b, carry):
+        got = jnp.dot(
+            ftr[...], taps[pl.ds(width, cells), pl.ds(pl.multiple_of(b * chans, 128), chans)],
+            preferred_element_type=F32,
+        )
+        kacc[0, rows_of(b * chans, chans, 16), :] = got[0:chans]
+        kgb[rows_of((3 + b) * chans, chans, 16), :] = got[chans:2 * chans].astype(BF)
+        kacc[1, rows_of(b * chans, chans, 16), :] = got[2 * chans:3 * chans]
+        return carry
+
+    lax.fori_loop(0, 3, ktap, 0)
+
+    loads[2].wait()
+    fsum = jnp.dot(fin[inner, :].T, fg[inner, :], preferred_element_type=F32)
 
     @pl.when(r > 0)
     def _():
@@ -210,46 +271,64 @@
     def _():
         halo[1] = jnp.zeros_like(halo[1])
 
-    spread(halo[0], 0)
-    spread(halo[1], strip + 1)
-    acc[...] += contract_last(shifted(0), wcat[0])
-    acc[...] += contract_last(shifted(2), wcat[2])
-
-    half = width // 2
-    lanes = [pl.ds(v * 128, 128) for v in range(chans // 128)]
-    for y in range(strip // 2):
-        pair = acc[pl.ds(2 * y * width, width), :] + acc[pl.ds((2 * y + 1) * width, width), :]
-        for v in range(chans // 128):
-            pool_f[v, pl.ds(y * width, width), :] = pair[:, v * 128:(v + 1) * 128]
-    mine = cells // 4
-    for v, lane in enumerate(lanes):
-        midg[r, :, lane] = (
-            pool_f[v, pl.ds(0, mine, stride=2), :] + pool_f[v, pl.ds(1, mine, stride=2), :]
-        ).astype(BF)
-    mids = []
-    for j in range(1, nr):
-        cp = remote(midg.at[r], midg.at[r], mid_s.at[j - 1], mid_r.at[j - 1],
-                    (d, lax.rem(r + j, nr)))
-        cp.start()
-        mids.append(cp)
-    fg[...] = acc[...].astype(BF)
-
-    loads[1].wait()
-    fine_t = fine[...].T
-    for a in range(3):
-        got = jnp.dot(fine_t, shifted(a), preferred_element_type=F32).astype(BF)
-        for b in range(3):
-            kgb[pl.ds((3 * a + b) * chans, chans), :] = got[:, b * chans:(b + 1) * chans]
-    loads[2].wait()
-    kgb[pl.ds(9 * chans, fin.shape[1]), :] = jnp.dot(
-        fin[...].T, fg[...], preferred_element_type=F32
-    ).astype(BF)
+    spread(halo[0], top_rim)
+    spread(halo[1], low_rim)
+    first, last = pl.ds(0, width), pl.ds(cells - width, width)
+    acc[first, :] += contract_last(taps[top_rim, :], wcat[2])
+    acc[last, :] += contract_last(taps[low_rim, :], wcat[0])
+    pool(0, 1)
+    pool(mrows - 1, 1)
+    send_mid(1, 0, 1)
+    send_mid(2, mrows - 1, 1)
+    fg[first, :] = acc[first, :].astype(BF)
+    fg[last, :] = acc[last, :].astype(BF)
+    rim0 = jnp.dot(fine[pl.ds(cells, width), :].T, taps[low_rim, :], preferred_element_type=F32)
+    rim2 = jnp.dot(fine[pl.ds(width, width), :].T, taps[top_rim, :], preferred_element_type=F32)
+    for b in range(3):
+        lane = slice(b * chans, (b + 1) * chans)
+        kgb[pl.ds(b * chans, chans), :] = (kacc[0, pl.ds(b * chans, chans), :] + rim0[:, lane]).astype(BF)
+        kgb[pl.ds((6 + b) * chans, chans), :] = (
+            kacc[1, pl.ds(b * chans, chans), :] + rim2[:, lane]).astype(BF)
+    fsum += jnp.dot(fin[first, :].T, fg[first, :], preferred_element_type=F32)
+    fsum += jnp.dot(fin[last, :].T, fg[last, :], preferred_element_type=F32)
+    kgb[pl.ds(9 * chans, fin.shape[1]), :] = fsum.astype(BF)
+
+    low = z < nz // 2
+    far = []
+    for k in range(nz - 1):
+        down_z = nz - 1 - k
+        zt = jnp.where(low, jnp.where(down_z > z, down_z, down_z - 1), jnp.where(k < z, k, k + 1))
+        far.append(zt)
+    far.append(z)
     firsts = []
-    for n in range(chips):
-        cp = remote(kgb.at[rows_of((2 * n + other) * share, share, 16)], ra.at[n],
-                    a_s.at[n], a_r.at[n], sibling)
-        cp.start()
-        firsts.append(cp)
+    for zt in far:
+        for i in range(nx):
+            n = zt * nx + i
+            cp = remote(kgb.at[rows_of((2 * n + other) * share, share, 16)], ra.at[n],
+                        a_s.at[n], a_r.at[n], sibling)
+            cp.start()
+            firsts.append((n, cp))
+
+    loads[3].wait()
+    gf[...] = contract_last(fg[...], lat_f[...]).astype(BF)
+    outs = [pltpu.make_async_copy(gf, gf_h, out_sem.at[0])]
+    outs[0].start()
+
+    seconds = []
+    for g, zt in enumerate(far):
+        for n, cp in firsts[g * nx:(g + 1) * nx]:
+            cp.wait_recv()
+            sb[n] = (
+                kgb[rows_of((2 * n + core) * share, share, 16), :].astype(F32) + ra[n].astype(F32)
+            ).astype(BF)
+        row = []
+        for n, (i, j) in enumerate(plane):
+            xt, rt = lax.rem(x + i, nx), lax.rem(r + j, nr)
+            cp = remote(sb.at[zt * nx + xt, rows_of(rt * part, part, 16)], rb.at[n, g],
+                        b_s.at[n, g], b_r.at[n, g], dev(z, xt, rt))
+            cp.start()
+            row.append(cp)
+        seconds.append((g, zt, row))
 
     for cp in mids:
         cp.wait_recv()
@@ -279,13 +358,6 @@
     chunk = per // chips
     cfirst = remote(ct.at[rows_of(other * per, per, 16)], rca, ca_s, ca_r, sibling)
     cfirst.start()
-
-    for n in range(chips):
-        firsts[n].wait_recv()
-        sb[n] = (
-            kgb[rows_of((2 * n + core) * share, share, 16), :].astype(F32) + ra[n].astype(F32)
-        ).astype(BF)
-
     cfirst.wait_recv()
     sc[...] = (
         ct[rows_of(core * per, per, 16), :].astype(F32) + rca[...].astype(F32)
@@ -298,23 +370,6 @@
         cp.start()
         cscat.append(cp)
 
-    order = list(range(1, nz)) + [0]
-    seconds = []
-    for t in order:
-        zt = lax.rem(z + t, nz)
-        row = []
-        for n, (i, j) in enumerate(plane):
-            xt, rt = lax.rem(x + i, nx), lax.rem(r + j, nr)
-            cp = remote(sb.at[zt * nx + xt, rows_of(rt * part, part, 16)], rb.at[n, t],
-                        b_s.at[n, t], b_r.at[n, t], dev(z, xt, rt))
-            cp.start()
-            row.append(cp)
-        seconds.append((t, zt, row))
-
-    loads[3].wait()
-    gf[...] = contract_last(fg[...], lat_f[...]).astype(BF)
-    outs = [pltpu.make_async_copy(gf, gf_h, out_sem.at[0])]
-    outs[0].start()
     loads[6].wait()
     gm[...] = contract_last(mflat, lat_m[...]).astype(BF)
     outs.append(pltpu.make_async_copy(gm, gm_h, out_sem.at[1]))
@@ -323,6 +378,17 @@
     gt[...] = contract_last(topg[...], lat_t[...]).astype(BF)
     outs.append(pltpu.make_async_copy(gt, gt_h, out_sem.at[2]))
     outs[2].start()
+
+    thirds = []
+    for g, zt, row in seconds[:-1]:
+        total = sb[zt * nx + x, rows_of(r * part, part, 16), :].astype(F32)
+        for n, cp in enumerate(row):
+            cp.wait_recv()
+            total += rb[n, g].astype(F32)
+        tb[g] = total.astype(BF)
+        cp = remote(tb.at[g], rc.at[z], c_s.at[g], c_r.at[z], dev(zt, x, r))
+        cp.start()
+        thirds.append(cp)
 
     total = sc[rows_of(q * chunk, chunk, 16), :].astype(F32)
     for k in range(1, chips):
@@ -338,21 +404,14 @@
         cp.start()
         cgath.append(cp)
 
-    thirds = []
-    for t, zt, row in seconds:
-        total = sb[zt * nx + x, rows_of(r * part, part, 16), :].astype(F32)
-        for n, cp in enumerate(row):
-            cp.wait_recv()
-            total += rb[n, t].astype(F32)
-        if t:
-            tb[t - 1] = total.astype(BF)
-            cp = remote(tb.at[t - 1], rc.at[t - 1], c_s.at[t - 1], c_r.at[t - 1],
-                        dev(zt, x, r))
-            cp.start()
-            thirds.append(cp)
-    for n, cp in enumerate(thirds):
+    total = sb[z * nx + x, rows_of(r * part, part, 16), :].astype(F32)
+    for n, cp in enumerate(seconds[-1][2]):
         cp.wait_recv()
-        total += rc[n].astype(F32)
+        total += rb[n, nz - 1].astype(F32)
+    for k in range(1, nz):
+        source = lax.rem(z + k, nz)
+        remote(tb.at[0], rc.at[source], c_s.at[0], c_r.at[source], dev(source, x, r)).wait_recv()
+        total += rc[source].astype(F32)
     spot = rows_of(r * part, part, 16)
     kf[spot, :] = total.astype(BF)
     lasts = []
@@ -383,7 +442,7 @@
     def _():
         up.wait_send()
 
-    sent = mids + firsts + [cfirst] + cscat + cgath + thirds + lasts + [ccore]
+    sent = mids + [cp for _, cp in firsts] + [cfirst] + cscat + cgath + thirds + lasts + [ccore]
     for _, _, row in seconds:
         sent += row
     for cp in sent:
@@ -439,21 +498,21 @@
     dma = pltpu.SemaphoreType.DMA
     vm = pltpu.VMEM
     scratch = [
-        vm((cells, chans), BF), vm((cells, chans), BF), vm((cells, cin), BF),
+        vm((cells, chans), BF), vm(((strip + 2) * width, chans), BF), vm((cells, cin), BF),
         vm((mcells, mc), BF), vm((tcells, tc), BF), vm((3, chans, 3 * chans), BF),
         vm((cin, chans), BF), vm((mc, chans), BF), vm((tc, chans), BF),
         vm((2, width, chans), BF), vm(((strip + 2) * width, 3 * chans), BF),
-        vm((cells, chans), F32), vm((cells, chans), BF), vm((chans // 128, cells // 2, 128), F32),
+        vm((3 * chans, cells), BF), vm((cells, chans), F32), vm((2, 3 * chans, chans), F32), vm((cells, chans), BF), vm((chans // 128, cells // 2, 128), F32),
         vm((nr, cells // 4, chans), BF), vm((chans // 128, mcells // 2, 128), F32), vm((tcells, chans), BF),
         vm((rows, chans), BF), vm((chips, share, chans), BF), vm((chips, share, chans), BF),
         vm((npl, nz, part, chans), BF), vm((nz - 1, part, chans), BF),
-        vm((nz - 1, part, chans), BF), vm((share, chans), BF),
+        vm((nz, part, chans), BF), vm((share, chans), BF),
         vm((2 * per, chans), BF), vm((per, chans), BF), vm((per, chans), BF),
         vm((chips - 1, chunk, chans), BF), vm((2 * per, chans), BF),
         vm((cells, cin), BF), vm((mcells, mc), BF), vm((tcells, tc), BF),
-        dma((8,)), dma((9,)), dma((5,)), dma((2,)), dma((2,)), dma((nr - 1,)), dma((nr - 1,)),
+        dma((8,)), dma((9,)), dma((5,)), dma((2,)), dma((2,)), dma((nr - 1, 3)), dma((nr - 1, 3)),
         dma((chips,)), dma((chips,)), dma((npl, nz)), dma((npl, nz)),
-        dma((nz - 1,)), dma((nz - 1,)), dma((nr - 1,)), dma((nr - 1,)),
+        dma((nz - 1,)), dma((nz,)), dma((nr - 1,)), dma((nr - 1,)),
         dma(()), dma(()), dma((chips - 1,)), dma((chips - 1,)),
         dma((chips - 1,)), dma((chips - 1,)), dma(()), dma(()),
     ]
@@ -509,7 +568,7 @@
     fits = (
         dp % 2 == 0 and images == 1 and nr > 1 and chips > nx
         and rows % (dp * nr * 16) == 0 and coarse % (dp * 16) == 0
-        and strip % 4 == 0 and width % 64 == 0 and chans % 128 == 0
+        and strip % 4 == 0 and strip >= 8 and width % 64 == 0 and chans % 128 == 0
     )
     if not fits:
         return plain_body(*args)

time: 36.5 us -> 33 us (0.904)
  Pallas kernels: 35.7 us -> 32 us
    pallas_call x1, Pallas kernels: 34.1 us -> 30.5 us  [kernel_body(): pl.pallas_call(functools.partial(fused, nz, nx, nr, strip, width), out_sh...]
where the time goes in v1:
time: 33 us; the launch traced here: 32.7 us
  Pallas kernels  32 us (97%)
  between operations  0.64 us (2%)
    pallas_call x1, Pallas kernels, kernel_body(): pl.pallas_call(functools.partial(fused, nz, nx, nr, strip, width), out_sh...  30.5 us
    pallas_call x1, Pallas kernels, kernel_body(): pl.pallas_call(put_out, out_shape=wide + final, in_specs=[anyspec] * 5, o...  1.6 us

profile of v1, /device:TPU:0, one launch (start us, length us, event | category | flops | bytes accessed | tf_op | source)
XLA Modules:
  0.0 32.7 jit_solution(2891147460553513293)
XLA Ops:
  0.6 30.5 %shard_map.136 = (bf16[1024,256]{1,0:T(8,128)(2,1)S(1)}, bf16[512,256]{1,0:T(8,128)(2,1)S(1)}, bf16[128,512]{1,0:T(8,128)(2,1)S(1)}, bf16[160,256]{1,0:T(8,128)(2,1)S(1)}, bf16[768,256]{1,0:T(8,128)(2,1)S(1)}) custom-call(bf16[1024,256]{1,0:T(8,128)(2,1)} %bitcast.8, bf16[1024,256]{1,0:T(8,128)(2,1)} %bitcast.9, bf16[1024,256]{1,0:T(8,128)(2,1)} %bitcast.10, ...), custom_call_target="tpu_custom_call" | custom-call | tf_op jit(solution)/shard_map/pallas_call | solution.py:531
  31.1 1.6 %shard_map.137 = (bf16[1024,256]{1,0:T(8,128)(2,1)}, bf16[512,256]{1,0:T(8,128)(2,1)}, bf16[128,512]{1,0:T(8,128)(2,1)}, f32[160,256]{1,0:T(8,128)}, f32[256,256]{1,0:T(8,128)}, /*index=5*/f32[512,256]{1,0:T(8,128)}) custom-call(bf16[1024,256]{1,0:T(8,128)(2,1)S(1)} %get-tuple-element.17.gf_i, bf16[512,256]{1,0:T(8,128)(2,1)S(1)} %get-tuple-element.18.gm_i, ...), custom_call_target="tpu_custom_call" | custom-call | tf_op jit(solution)/shard_map/pallas_call | solution.py:545

commit v2 on v1

--- a/solution.py
+++ b/solution.py
@@ -105,7 +105,7 @@
     gf, gm, gt,
     in_sem, w_sem, out_sem, halo_s, halo_r, mid_s, mid_r,
     a_s, a_r, b_s, b_r, c_s, c_r, d_s, d_r,
-    ca_s, ca_r, cs_s, cs_r, cg_s, cg_r, cc_s, cc_r,
+    ca_s, ca_r, cs_s, cs_r, cg_s, cg_r, cc_s, cc_r, relay,
 ):
     chips = nz * nx
     d = lax.axis_index("dp")
@@ -149,14 +149,29 @@
 
     barrier = pltpu.get_barrier_semaphore()
     plane = [(i, j) for i in range(nx) for j in range(nr) if (i, j) != (0, 0)]
-    greet = [sibling]
-    for k in range(1, chips):
-        greet.append((lax.rem(q + k, chips) * 2 + core, r))
-    for i, j in plane:
-        if j:
-            greet.append(dev(z, lax.rem(x + i, nx), lax.rem(r + j, nr)))
-    for to in greet:
-        pl.semaphore_signal(barrier, inc=1, device_id=to, device_id_type=MESH)
+    near = []
+    for low_end, high_end, before, after in (
+        (z > 0, z < nz - 1, dev(jnp.maximum(z - 1, 0), x, r), dev(jnp.minimum(z + 1, nz - 1), x, r)),
+        (x > 0, x < nx - 1, dev(z, jnp.maximum(x - 1, 0), r), dev(z, jnp.minimum(x + 1, nx - 1), r)),
+        (r > 0, r < nr - 1, dev(z, x, jnp.maximum(r - 1, 0)), dev(z, x, jnp.minimum(r + 1, nr - 1))),
+    ):
+        near += [(low_end, before), (high_end, after)]
+    nearby = sum(there.astype(jnp.int32) for there, _ in near)
+
+    def greet(sem):
+        for there, to in near:
+            @pl.when(there)
+            def _():
+                pl.semaphore_signal(sem, inc=1, device_id=to, device_id_type=MESH)
+
+    def hear(k):
+        pl.semaphore_wait(relay.at[k], nearby)
+        if k + 1 < relays:
+            greet(relay.at[k + 1])
+
+    relays = relay.shape[0]
+    pl.semaphore_signal(barrier, inc=1, device_id=sibling, device_id_type=MESH)
+    greet(barrier)
 
     top_rim, low_rim = pl.ds(0, width), pl.ds((strip + 1) * width, width)
     taps[top_rim, :] = jnp.zeros((width, 3 * chans), BF)
@@ -175,7 +190,19 @@
         taps[here, 2 * chans:3 * chans] = before.astype(BF)
 
     loads[0].wait()
-    pl.semaphore_wait(barrier, len(greet))
+    def spread_row(y, carry):
+        spread(og[rows_of(y * width, width, width), :], rows_of((y + 1) * width, width, width))
+        return carry
+
+    lax.fori_loop(0, strip, spread_row, 0)
+    loads[1].wait()
+    wide_t = fine[...].T
+    ftr[pl.ds(0, chans), :] = wide_t[:, 0:cells]
+    ftr[pl.ds(chans, chans), :] = fine[pl.ds(width, cells), :].T
+    ftr[pl.ds(2 * chans, chans), :] = wide_t[:, 2 * width:2 * width + cells]
+
+    pl.semaphore_wait(barrier, nearby + 1)
+    greet(relay.at[0])
     down = remote(og.at[pl.ds(cells - width, width)], halo.at[0], halo_s.at[0], halo_r.at[0],
                   (d, lax.rem(r + 1, nr)))
     up = remote(og.at[pl.ds(0, width)], halo.at[1], halo_s.at[1], halo_r.at[1],
@@ -189,11 +216,6 @@
     def _():
         up.start()
 
-    def spread_row(y, carry):
-        spread(og[rows_of(y * width, width, width), :], rows_of((y + 1) * width, width, width))
-        return carry
-
-    lax.fori_loop(0, strip, spread_row, 0)
     for cp in wloads:
         cp.wait()
 
@@ -202,56 +224,56 @@
     level += contract_last(taps[pl.ds(0, cells), :], wcat[2])
     acc[...] = level
 
+    hear(0)
     half = width // 2
     mine = cells // 4
     lanes = [pl.ds(v * 128, 128) for v in range(chans // 128)]
 
     def pool(y0, count):
-        for y in range(y0, y0 + count):
-            pair = acc[pl.ds(2 * y * width, width), :] + acc[pl.ds((2 * y + 1) * width, width), :]
+        for y in range(count):
+            at = 2 * (y0 + y) * width
+            pair = acc[rows_of(at, width, width), :] + acc[rows_of(at + width, width, width), :]
             for v in range(chans // 128):
                 pool_f[v, pl.ds(y * width, width), :] = pair[:, v * 128:(v + 1) * 128]
         for v, lane in enumerate(lanes):
-            midg[r, pl.ds(y0 * half, count * half), lane] = (
-                pool_f[v, pl.ds(y0 * width, count * half, stride=2), :]
-                + pool_f[v, pl.ds(y0 * width + 1, count * half, stride=2), :]
+            midg[r, rows_of(y0 * half, count * half, 16), lane] = (
+                pool_f[v, pl.ds(0, count * half, stride=2), :]
+                + pool_f[v, pl.ds(1, count * half, stride=2), :]
             ).astype(BF)
 
     mrows = strip // 2
-    pool(1, mrows - 2)
+    pool(0, mrows)
+    rims = [r] if nr == 2 else [0, 1]
+    start = r if nr == 2 else 1
+    count = mrows - len(rims)
     mids = []
 
     def send_mid(e, y0, count):
-        here = midg.at[r, pl.ds(y0 * half, count * half)]
+        here = midg.at[r, rows_of(y0 * half, count * half, 16)]
         for j in range(1, nr):
             cp = remote(here, here, mid_s.at[j - 1, e], mid_r.at[j - 1, e],
                         (d, lax.rem(r + j, nr)))
             cp.start()
             mids.append(cp)
 
-    send_mid(0, 1, mrows - 2)
-
-    inner = pl.ds(width, cells - 2 * width)
-    fg[inner, :] = acc[inner, :].astype(BF)
-
-    loads[1].wait()
-    wide_t = fine[...].T
-    ftr[pl.ds(0, chans), :] = wide_t[:, 0:cells]
-    ftr[pl.ds(chans, chans), :] = fine[pl.ds(width, cells), :].T
-    ftr[pl.ds(2 * chans, chans), :] = wide_t[:, 2 * width:2 * width + cells]
+    send_mid(0, start, count)
+    inner = rows_of(start * width, cells - len(rims) * width, width)
+    fg[...] = acc[...].astype(BF)
 
     def ktap(b, carry):
         got = jnp.dot(
             ftr[...], taps[pl.ds(width, cells), pl.ds(pl.multiple_of(b * chans, 128), chans)],
             preferred_element_type=F32,
         )
+        for a in range(3):
+            kgb[rows_of((3 * a + b) * chans, chans, 16), :] = got[a * chans:(a + 1) * chans].astype(BF)
         kacc[0, rows_of(b * chans, chans, 16), :] = got[0:chans]
-        kgb[rows_of((3 + b) * chans, chans, 16), :] = got[chans:2 * chans].astype(BF)
         kacc[1, rows_of(b * chans, chans, 16), :] = got[2 * chans:3 * chans]
         return carry
 
     lax.fori_loop(0, 3, ktap, 0)
 
+    hear(1)
     loads[2].wait()
     fsum = jnp.dot(fin[inner, :].T, fg[inner, :], preferred_element_type=F32)
 
@@ -259,40 +281,43 @@
     def _():
         down.wait_recv()
 
-    @pl.when(r == 0)
-    def _():
-        halo[0] = jnp.zeros_like(halo[0])
-
     @pl.when(r < nr - 1)
     def _():
         up.wait_recv()
 
-    @pl.when(r == nr - 1)
-    def _():
-        halo[1] = jnp.zeros_like(halo[1])
-
-    spread(halo[0], top_rim)
-    spread(halo[1], low_rim)
-    first, last = pl.ds(0, width), pl.ds(cells - width, width)
-    acc[first, :] += contract_last(taps[top_rim, :], wcat[2])
-    acc[last, :] += contract_last(taps[low_rim, :], wcat[0])
-    pool(0, 1)
-    pool(mrows - 1, 1)
-    send_mid(1, 0, 1)
-    send_mid(2, mrows - 1, 1)
-    fg[first, :] = acc[first, :].astype(BF)
-    fg[last, :] = acc[last, :].astype(BF)
-    rim0 = jnp.dot(fine[pl.ds(cells, width), :].T, taps[low_rim, :], preferred_element_type=F32)
-    rim2 = jnp.dot(fine[pl.ds(width, width), :].T, taps[top_rim, :], preferred_element_type=F32)
-    for b in range(3):
-        lane = slice(b * chans, (b + 1) * chans)
-        kgb[pl.ds(b * chans, chans), :] = (kacc[0, pl.ds(b * chans, chans), :] + rim0[:, lane]).astype(BF)
-        kgb[pl.ds((6 + b) * chans, chans), :] = (
-            kacc[1, pl.ds(b * chans, chans), :] + rim2[:, lane]).astype(BF)
-    fsum += jnp.dot(fin[first, :].T, fg[first, :], preferred_element_type=F32)
-    fsum += jnp.dot(fin[last, :].T, fg[last, :], preferred_element_type=F32)
+    if nr > 2:
+        @pl.when(r == 0)
+        def _():
+            halo[0] = jnp.zeros_like(halo[0])
+
+        @pl.when(r == nr - 1)
+        def _():
+            halo[1] = jnp.zeros_like(halo[1])
+
+    def mend(n, e):
+        rim = rows_of((1 - e) * (strip + 1) * width, width, width)
+        edge = rows_of((1 - e) * (cells - width), width, width)
+        mate = rows_of((1 - e) * (cells - width) + width, width, width)
+        y0 = (1 - e) * (mrows - 1)
+        spread(halo[1 - e], rim)
+        acc[edge, :] += contract_last(taps[rim, :], wcat[2 * e])
+        pool(y0, 1)
+        send_mid(1 + n, y0, 1)
+        fg[edge, :] = acc[edge, :].astype(BF)
+        more = jnp.dot(fine[mate, :].T, taps[rim, :], preferred_element_type=F32)
+        for b in range(3):
+            kgb[rows_of((6 * e + b) * chans, chans, 16), :] = (
+                kacc[e, pl.ds(b * chans, chans), :] + more[:, b * chans:(b + 1) * chans]
+            ).astype(BF)
+        return edge
+
+    for n, e in enumerate(rims):
+        edge = mend(n, e)
+        fsum += jnp.dot(fin[edge, :].T, fg[edge, :], preferred_element_type=F32)
     kgb[pl.ds(9 * chans, fin.shape[1]), :] = fsum.astype(BF)
 
+    for k in range(2, relays):
+        hear(k)
     low = z < nz // 2
     far = []
     for k in range(nz - 1):
@@ -315,20 +340,28 @@
     outs[0].start()
 
     seconds = []
-    for g, zt in enumerate(far):
+
+    def sum_group(g):
         for n, cp in firsts[g * nx:(g + 1) * nx]:
             cp.wait_recv()
             sb[n] = (
                 kgb[rows_of((2 * n + core) * share, share, 16), :].astype(F32) + ra[n].astype(F32)
             ).astype(BF)
+
+    def send_group(g):
         row = []
         for n, (i, j) in enumerate(plane):
             xt, rt = lax.rem(x + i, nx), lax.rem(r + j, nr)
-            cp = remote(sb.at[zt * nx + xt, rows_of(rt * part, part, 16)], rb.at[n, g],
+            cp = remote(sb.at[far[g] * nx + xt, rows_of(rt * part, part, 16)], rb.at[n, g],
                         b_s.at[n, g], b_r.at[n, g], dev(z, xt, rt))
             cp.start()
             row.append(cp)
-        seconds.append((g, zt, row))
+        seconds.append((g, far[g], row))
+
+    ahead = nz // 2
+    for g in range(ahead):
+        sum_group(g)
+        send_group(g)
 
     for cp in mids:
         cp.wait_recv()
@@ -358,6 +391,8 @@
     chunk = per // chips
     cfirst = remote(ct.at[rows_of(other * per, per, 16)], rca, ca_s, ca_r, sibling)
     cfirst.start()
+    for g in range(ahead, nz):
+        sum_group(g)
     cfirst.wait_recv()
     sc[...] = (
         ct[rows_of(core * per, per, 16), :].astype(F32) + rca[...].astype(F32)
@@ -369,6 +404,9 @@
                     cs_s.at[k - 1], cs_r.at[k - 1], (to * 2 + core, r))
         cp.start()
         cscat.append(cp)
+
+    for g in range(ahead, nz):
+        send_group(g)
 
     loads[6].wait()
     gm[...] = contract_last(mflat, lat_m[...]).astype(BF)
@@ -515,6 +553,7 @@
         dma((nz - 1,)), dma((nz,)), dma((nr - 1,)), dma((nr - 1,)),
         dma(()), dma(()), dma((chips - 1,)), dma((chips - 1,)),
         dma((chips - 1,)), dma((chips - 1,)), dma(()), dma(()),
+        pltpu.SemaphoreType.REGULAR((max(nz + nx, nx + nr) - 3,)),
     ]
     hbm = pl.BlockSpec(memory_space=pltpu.HBM)
     anyspec = pl.BlockSpec(memory_space=pl.ANY)
@@ -566,7 +605,7 @@
     rows = 9 * chans + fine_input.shape[-1]
     coarse = mid_input.shape[-1] + top_input.shape[-1]
     fits = (
-        dp % 2 == 0 and images == 1 and nr > 1 and chips > nx
+        dp % 2 == 0 and images == 1 and nr > 1 and chips > nx > 1 and chips // nx > 2
         and rows % (dp * nr * 16) == 0 and coarse % (dp * 16) == 0
         and strip % 4 == 0 and strip >= 8 and width % 64 == 0 and chans % 128 == 0
     )

time: 33 us -> 31.2 us (0.945)
  Pallas kernels: 32 us -> 30.3 us
    pallas_call x1, Pallas kernels: 30.5 us -> 28.7 us  [kernel_body(): pl.pallas_call(functools.partial(fused, nz, nx, nr, strip, width), out_sh...]
where the time goes in v2:
time: 31.2 us; the launch traced here: 30.9 us
  Pallas kernels  30.3 us (97%)
  between operations  0.64 us (2%)
    pallas_call x1, Pallas kernels, kernel_body(): pl.pallas_call(functools.partial(fused, nz, nx, nr, strip, width), out_sh...  28.7 us
    pallas_call x1, Pallas kernels, kernel_body(): pl.pallas_call(put_out, out_shape=wide + final, in_specs=[anyspec] * 5, o...  1.6 us

profile of v2, /device:TPU:0, one launch (start us, length us, event | category | flops | bytes accessed | tf_op | source)
XLA Modules:
  0.0 30.9 jit_solution(8277565062634306490)
XLA Ops:
  0.6 28.7 %shard_map.136 = (bf16[1024,256]{1,0:T(8,128)(2,1)S(1)}, bf16[512,256]{1,0:T(8,128)(2,1)S(1)}, bf16[128,512]{1,0:T(8,128)(2,1)S(1)}, bf16[160,256]{1,0:T(8,128)(2,1)S(1)}, bf16[768,256]{1,0:T(8,128)(2,1)S(1)}) custom-call(bf16[1024,256]{1,0:T(8,128)(2,1)} %bitcast.8, bf16[1024,256]{1,0:T(8,128)(2,1)} %bitcast.9, bf16[1024,256]{1,0:T(8,128)(2,1)} %bitcast.10, ...), custom_call_target="tpu_custom_call" | custom-call | tf_op jit(solution)/shard_map/pallas_call | solution.py:570
  29.3 1.6 %shard_map.137 = (bf16[1024,256]{1,0:T(8,128)(2,1)}, bf16[512,256]{1,0:T(8,128)(2,1)}, bf16[128,512]{1,0:T(8,128)(2,1)}, f32[160,256]{1,0:T(8,128)}, f32[256,256]{1,0:T(8,128)}, /*index=5*/f32[512,256]{1,0:T(8,128)}) custom-call(bf16[1024,256]{1,0:T(8,128)(2,1)S(1)} %get-tuple-element.17.gf_i, bf16[512,256]{1,0:T(8,128)(2,1)S(1)} %get-tuple-element.18.gm_i, ...), custom_call_target="tpu_custom_call" | custom-call | tf_op jit(solution)/shard_map/pallas_call | solution.py:584

commit v3 on v2

--- a/solution.py
+++ b/solution.py
@@ -102,8 +102,7 @@
     halo, taps, ftr, acc, kacc, fg, pool_f, midg, topf, topg,
     kgb, ra, sb, rb, tb, rc, kf,
     ct, rca, sc, rcs, gath,
-    gf, gm, gt,
-    in_sem, w_sem, out_sem, halo_s, halo_r, mid_s, mid_r,
+    in_sem, w_sem, halo_s, halo_r, mid_s, mid_r,
     a_s, a_r, b_s, b_r, c_s, c_r, d_s, d_r,
     ca_s, ca_r, cs_s, cs_r, cg_s, cg_r, cc_s, cc_r, relay,
 ):
@@ -335,9 +334,7 @@
             firsts.append((n, cp))
 
     loads[3].wait()
-    gf[...] = contract_last(fg[...], lat_f[...]).astype(BF)
-    outs = [pltpu.make_async_copy(gf, gf_h, out_sem.at[0])]
-    outs[0].start()
+    gf_h[...] = contract_last(fg[...], lat_f[...]).astype(BF)
 
     seconds = []
 
@@ -358,7 +355,7 @@
             row.append(cp)
         seconds.append((g, far[g], row))
 
-    ahead = nz // 2
+    ahead = nz - 1
     for g in range(ahead):
         sum_group(g)
         send_group(g)
@@ -409,13 +406,9 @@
         send_group(g)
 
     loads[6].wait()
-    gm[...] = contract_last(mflat, lat_m[...]).astype(BF)
-    outs.append(pltpu.make_async_copy(gm, gm_h, out_sem.at[1]))
-    outs[1].start()
+    gm_h[...] = contract_last(mflat, lat_m[...]).astype(BF)
     loads[7].wait()
-    gt[...] = contract_last(topg[...], lat_t[...]).astype(BF)
-    outs.append(pltpu.make_async_copy(gt, gt_h, out_sem.at[2]))
-    outs[2].start()
+    gt_h[...] = contract_last(topg[...], lat_t[...]).astype(BF)
 
     thirds = []
     for g, zt, row in seconds[:-1]:
@@ -434,6 +427,11 @@
         total += rcs[k - 1].astype(F32)
     place = core * per + q * chunk
     gath[rows_of(place, chunk, 16), :] = total.astype(BF)
+
+    def hand_over(k):
+        held = gath.at[rows_of(core * per + lax.rem(q + chips - k, chips) * chunk, chunk, 16)]
+        return remote(held, held, cc_s.at[k], cc_r.at[k], sibling)
+
     cgath = []
     for k in range(1, chips):
         here = rows_of(place, chunk, 16)
@@ -441,6 +439,7 @@
                     (lax.rem(q + k, chips) * 2 + core, r))
         cp.start()
         cgath.append(cp)
+    hand_over(0).start()
 
     total = sb[z * nx + x, rows_of(r * part, part, 16), :].astype(F32)
     for n, cp in enumerate(seconds[-1][2]):
@@ -459,18 +458,18 @@
         cp.start()
         lasts.append(cp)
 
-    for cp in cgath:
-        cp.wait_recv()
-    block = rows_of(core * per, per, 16)
-    ccore = remote(gath.at[block], gath.at[block], cc_s, cc_r, sibling)
-    ccore.start()
+    for k in range(1, chips):
+        cgath[k - 1].wait_recv()
+        hand_over(k).start()
     for cp in lasts:
         cp.wait_recv()
-    outs.append(pltpu.make_async_copy(kf, kf_h, out_sem.at[3]))
-    outs[3].start()
-    ccore.wait_recv()
-    outs.append(pltpu.make_async_copy(gath, ga_h, out_sem.at[4]))
-    outs[4].start()
+    kf_h[...] = kf[...].astype(F32)
+    block = rows_of(core * per, per, 16)
+    ga_h[block, :] = gath[block, :].astype(F32)
+    for k in range(chips):
+        hand_over(k).wait_recv()
+    rest = rows_of(other * per, per, 16)
+    ga_h[rest, :] = gath[rest, :].astype(F32)
 
     @pl.when(r < nr - 1)
     def _():
@@ -480,40 +479,22 @@
     def _():
         up.wait_send()
 
-    sent = mids + [cp for _, cp in firsts] + [cfirst] + cscat + cgath + thirds + lasts + [ccore]
+    sent = mids + [cp for _, cp in firsts] + [cfirst] + cscat + cgath + thirds + lasts + [hand_over(k) for k in range(chips)]
     for _, _, row in seconds:
         sent += row
     for cp in sent:
         cp.wait_send()
-    for cp in outs:
-        cp.wait()
-
-
-def put_out(gf_i, gm_i, gt_i, kf_i, ga_i, gf_o, gm_o, gt_o, kg_o, ml_o, tl_o,
-            kf, ga, kg, ml, tl, in_sem, out_sem):
-    loads = [
-        pltpu.make_async_copy(src, dst, in_sem.at[n])
-        for n, (src, dst) in enumerate(
-            ((ga_i, ga), (kf_i, kf)))
-    ]
-    for cp in loads:
+
+
+def put_out(gf_i, gm_i, gt_i, kg_i, ga_i, gf_o, gm_o, gt_o, kg_o, ml_o, tl_o, out_sem):
+    mc = ml_o.shape[0]
+    pairs = (
+        (ga_i.at[pl.ds(mc, tl_o.shape[0])], tl_o), (gf_i, gf_o), (ga_i.at[pl.ds(0, mc)], ml_o),
+        (gm_i, gm_o), (kg_i, kg_o), (gt_i, gt_o),
+    )
+    stores = [pltpu.make_async_copy(src, dst, out_sem.at[n]) for n, (src, dst) in enumerate(pairs)]
+    for cp in stores:
         cp.start()
-    stores = [
-        pltpu.make_async_copy(src, dst, out_sem.at[n])
-        for n, (src, dst) in enumerate(
-            ((gf_i, gf_o), (gm_i, gm_o), (gt_i, gt_o), (kg, kg_o), (ml, ml_o), (tl, tl_o)))
-    ]
-    for n in range(3):
-        stores[n].start()
-    loads[1].wait()
-    kg[...] = kf[...].astype(F32)
-    stores[3].start()
-    loads[0].wait()
-    mc = ml.shape[0]
-    ml[...] = ga[pl.ds(0, mc), :].astype(F32)
-    stores[4].start()
-    tl[...] = ga[pl.ds(mc, tl.shape[0]), :].astype(F32)
-    stores[5].start()
     for cp in stores:
         cp.wait()
 
@@ -547,21 +528,20 @@
         vm((nz, part, chans), BF), vm((share, chans), BF),
         vm((2 * per, chans), BF), vm((per, chans), BF), vm((per, chans), BF),
         vm((chips - 1, chunk, chans), BF), vm((2 * per, chans), BF),
-        vm((cells, cin), BF), vm((mcells, mc), BF), vm((tcells, tc), BF),
-        dma((8,)), dma((9,)), dma((5,)), dma((2,)), dma((2,)), dma((nr - 1, 3)), dma((nr - 1, 3)),
+        dma((8,)), dma((9,)), dma((2,)), dma((2,)), dma((nr - 1, 3)), dma((nr - 1, 3)),
         dma((chips,)), dma((chips,)), dma((npl, nz)), dma((npl, nz)),
         dma((nz - 1,)), dma((nz,)), dma((nr - 1,)), dma((nr - 1,)),
         dma(()), dma(()), dma((chips - 1,)), dma((chips - 1,)),
-        dma((chips - 1,)), dma((chips - 1,)), dma(()), dma(()),
+        dma((chips - 1,)), dma((chips - 1,)), dma((chips,)), dma((chips,)),
         pltpu.SemaphoreType.REGULAR((max(nz + nx, nx + nr) - 3,)),
     ]
     hbm = pl.BlockSpec(memory_space=pltpu.HBM)
-    anyspec = pl.BlockSpec(memory_space=pl.ANY)
+    inner = pl.BlockSpec(memory_space=pltpu.VMEM)
     wide = [
         jax.ShapeDtypeStruct((cells, cin), BF), jax.ShapeDtypeStruct((mcells, mc), BF),
         jax.ShapeDtypeStruct((tcells, tc), BF),
     ]
-    held = [jax.ShapeDtypeStruct((share, chans), BF), jax.ShapeDtypeStruct((2 * per, chans), BF)]
+    held = [jax.ShapeDtypeStruct((share, chans), F32), jax.ShapeDtypeStruct((2 * per, chans), F32)]
     final = [
         jax.ShapeDtypeStruct((share, chans), F32), jax.ShapeDtypeStruct((mc, chans), F32),
         jax.ShapeDtypeStruct((tc, chans), F32),
@@ -571,7 +551,7 @@
         functools.partial(fused, nz, nx, nr, strip, width),
         out_shape=[pltpu.VMEM(o.shape, o.dtype) for o in wide + held],
         in_specs=[hbm] * 9,
-        out_specs=[anyspec] * 5,
+        out_specs=[inner] * 5,
         scratch_shapes=scratch,
         compiler_params=pltpu.CompilerParams(
             collective_id=0, has_side_effects=True, vmem_limit_bytes=48 * 1024 * 1024
@@ -584,10 +564,9 @@
     gf, gm, gt, kg, ml, tl = pl.pallas_call(
         put_out,
         out_shape=wide + final,
-        in_specs=[anyspec] * 5,
+        in_specs=[inner] * 5,
         out_specs=[hbm] * 6,
-        scratch_shapes=[vm(o.shape, o.dtype) for o in held + final]
-        + [dma((2,)), dma((6,))],
+        scratch_shapes=[dma((6,))],
         compiler_params=pltpu.CompilerParams(vmem_limit_bytes=8 * 1024 * 1024),
     )(*between)
     return (

time: 31.2 us -> 30.3 us (0.971)
  Pallas kernels: 30.3 us -> 29.5 us
    pallas_call x1, Pallas kernels: 28.7 us -> 28.2 us  [kernel_body(): pl.pallas_call(functools.partial(fused, nz, nx, nr, strip, width), out_sh...]
    pallas_call x1, Pallas kernels: 1.6 us -> 1.28 us  [kernel_body(): pl.pallas_call(put_out, out_shape=wide + final, in_specs=[inner] * 5, out...]
where the time goes in v3:
time: 30.3 us; the launch traced here: 30.1 us
  Pallas kernels  29.5 us (97%)
  between operations  0.64 us (2%)
    pallas_call x1, Pallas kernels, kernel_body(): pl.pallas_call(functools.partial(fused, nz, nx, nr, strip, width), out_sh...  28.2 us
    pallas_call x1, Pallas kernels, kernel_body(): pl.pallas_call(put_out, out_shape=wide + final, in_specs=[inner] * 5, out...  1.28 us

profile of v3, /device:TPU:0, one launch (start us, length us, event | category | flops | bytes accessed | tf_op | source)
XLA Modules:
  0.0 30.1 jit_solution(14812163284993835321)
XLA Ops:
  0.6 28.2 %shard_map.136 = (bf16[1024,256]{1,0:T(8,128)(2,1)S(1)}, bf16[512,256]{1,0:T(8,128)(2,1)S(1)}, bf16[128,512]{1,0:T(8,128)(2,1)S(1)}, f32[160,256]{1,0:T(8,128)S(1)}, f32[768,256]{1,0:T(8,128)S(1)}) custom-call(bf16[1024,256]{1,0:T(8,128)(2,1)} %bitcast.8, bf16[1024,256]{1,0:T(8,128)(2,1)} %bitcast.9, bf16[1024,256]{1,0:T(8,128)(2,1)} %bitcast.10, ...), custom_call_target="tpu_custom_call" | custom-call | tf_op jit(solution)/shard_map/pallas_call | solution.py:550
  28.8 1.3 %shard_map.137 = (bf16[1024,256]{1,0:T(8,128)(2,1)}, bf16[512,256]{1,0:T(8,128)(2,1)}, bf16[128,512]{1,0:T(8,128)(2,1)}, f32[160,256]{1,0:T(8,128)}, f32[256,256]{1,0:T(8,128)}, /*index=5*/f32[512,256]{1,0:T(8,128)}) custom-call(bf16[1024,256]{1,0:T(8,128)(2,1)S(1)} %get-tuple-element.17.gf_i, bf16[512,256]{1,0:T(8,128)(2,1)S(1)} %get-tuple-element.18.gm_i, ...), custom_call_target="tpu_custom_call" | custom-call | tf_op jit(solution)/shard_map/pallas_call | solution.py:564

commit v4 on v3

--- a/solution.py
+++ b/solution.py
@@ -141,10 +141,6 @@
                 w_h.at[a, b], wcat.at[a, :, b * chans:(b + 1) * chans], w_sem.at[3 * a + b]
             ))
     loads[0].start()
-    for cp in wloads:
-        cp.start()
-    for cp in loads[1:]:
-        cp.start()
 
     barrier = pltpu.get_barrier_semaphore()
     plane = [(i, j) for i in range(nx) for j in range(nr) if (i, j) != (0, 0)]
@@ -172,6 +168,12 @@
     pl.semaphore_signal(barrier, inc=1, device_id=sibling, device_id_type=MESH)
     greet(barrier)
 
+    loads[1].start()
+    for cp in wloads:
+        cp.start()
+    for cp in loads[2:]:
+        cp.start()
+
     top_rim, low_rim = pl.ds(0, width), pl.ds((strip + 1) * width, width)
     taps[top_rim, :] = jnp.zeros((width, 3 * chans), BF)
     taps[low_rim, :] = jnp.zeros((width, 3 * chans), BF)
@@ -222,6 +224,7 @@
     level += contract_last(taps[pl.ds(width, cells), :], wcat[1])
     level += contract_last(taps[pl.ds(0, cells), :], wcat[2])
     acc[...] = level
+    fg[...] = level.astype(BF)
 
     hear(0)
     half = width // 2
@@ -257,7 +260,6 @@
 
     send_mid(0, start, count)
     inner = rows_of(start * width, cells - len(rims) * width, width)
-    fg[...] = acc[...].astype(BF)
 
     def ktap(b, carry):
         got = jnp.dot(

time: 30.3 us -> 30.1 us (level)
  no operation moved by 1% of the time
where the time goes in v4:
time: 30.1 us; the launch traced here: 29.9 us
  Pallas kernels  29.3 us (97%)
  between operations  0.64 us (2%)
    pallas_call x1, Pallas kernels, kernel_body(): pl.pallas_call(functools.partial(fused, nz, nx, nr, strip, width), out_sh...  28 us
    pallas_call x1, Pallas kernels, kernel_body(): pl.pallas_call(put_out, out_shape=wide + final, in_specs=[inner] * 5, out...  1.28 us

profile of v4, /device:TPU:0, one launch (start us, length us, event | category | flops | bytes accessed | tf_op | source)
XLA Modules:
  0.0 29.9 jit_solution(15330110570441852801)
XLA Ops:
  0.6 28.0 %shard_map.136 = (bf16[1024,256]{1,0:T(8,128)(2,1)S(1)}, bf16[512,256]{1,0:T(8,128)(2,1)S(1)}, bf16[128,512]{1,0:T(8,128)(2,1)S(1)}, f32[160,256]{1,0:T(8,128)S(1)}, f32[768,256]{1,0:T(8,128)S(1)}) custom-call(bf16[1024,256]{1,0:T(8,128)(2,1)} %bitcast.8, bf16[1024,256]{1,0:T(8,128)(2,1)} %bitcast.9, bf16[1024,256]{1,0:T(8,128)(2,1)} %bitcast.10, ...), custom_call_target="tpu_custom_call" | custom-call | tf_op jit(solution)/shard_map/pallas_call | solution.py:552
  28.7 1.3 %shard_map.137 = (bf16[1024,256]{1,0:T(8,128)(2,1)}, bf16[512,256]{1,0:T(8,128)(2,1)}, bf16[128,512]{1,0:T(8,128)(2,1)}, f32[160,256]{1,0:T(8,128)}, f32[256,256]{1,0:T(8,128)}, /*index=5*/f32[512,256]{1,0:T(8,128)}) custom-call(bf16[1024,256]{1,0:T(8,128)(2,1)S(1)} %get-tuple-element.17.gf_i, bf16[512,256]{1,0:T(8,128)(2,1)S(1)} %get-tuple-element.18.gm_i, ...), custom_call_target="tpu_custom_call" | custom-call | tf_op jit(solution)/shard_map/pallas_call | solution.py:566
